TPU v7x, 32 devices: a whole 2x2x4 slice. The times are simulated.
32 devices in a mesh: row: 8 (over y, x, core), col: 4 (over z).
Axes of the slice: x: 2, y: 2, z: 4, core: 2. Of those that a mesh axis runs over, the one named last changes fastest.
Arguments:
- signal: float32 [128, 128, 16, 256], P('row', 'col'), may hold values from -40 to 40, as said below
- start_frames: float32 [256, 32], replicated, may hold values from -6 to 6
- start_sends: float32 [16, 8], replicated, may hold values from -6 to 6
- start_rows: float32 [128, 64], replicated, may hold values from -6 to 6
- start_cols: float32 [128, 64], replicated, may hold values from -6 to 6
- rank_frames: int32 [1], replicated, may hold values from 16 to 32
- rank_sends: int32 [1], replicated, may hold values from 4 to 8
Outputs:
- filtered: float32 [128, 128, 16, 256], P('row', 'col')
Inputs may be any that keep to these rules, and one draw needn't show every extreme that they name: `signal`: beamformed samples.
All inputs are finite; a program needn't handle non-finite values.
Results may differ from a plain program's by a relative error of at most 0.0003.
Values sent between devices are 32-bit elements; how exact they have to be, the bound alone decides.
No kernel may reach another device: no remote copies, remote signals or barrier semaphores. Data moves between devices by JAX's collectives and lax.ppermute only.
A program may use at most 128 MiB of HBM per device.

v0:
```python
import jax
import jax.numpy as jnp
from jax import lax
from jax.sharding import PartitionSpec as P

NT = 256
NK = 16
TMAX = 32
KMAX = 8
RS = 64
ITERS = 2
CORE_W = 256


def orthonormal(gram, start):
    high = lax.Precision.HIGHEST
    basis = start
    for rounds in range(ITERS):
        image = jnp.dot(gram, basis, precision=high)
        inner = jnp.dot(image.T, image, precision=high)
        factor = jnp.linalg.cholesky(inner)
        basis = jax.scipy.linalg.solve_triangular(factor, image.T, lower=True).T
    return basis


def local(signal, start_frames, start_sends, start_rows, start_cols, rank_frames, rank_sends):
    high = lax.Precision.HIGHEST
    rows_dev, cols_dev = (signal.shape[0], signal.shape[1])
    pixels = rows_dev * cols_dev
    flattened = signal.reshape(-1, NT)
    blocks = signal.reshape(pixels, NK, NT)
    local_frames = jnp.einsum("pt,pu->tu", flattened, flattened, precision=high)
    local_sends = jnp.einsum("pkt,pjt->kj", blocks, blocks, precision=high)
    gram_frames, gram_sends = lax.psum((local_frames, local_sends), ("row", "col"))
    keep_frames = (jnp.arange(TMAX, dtype=jnp.int32) < rank_frames[0]).astype(jnp.float32)
    keep_sends = (jnp.arange(KMAX, dtype=jnp.int32) < rank_sends[0]).astype(jnp.float32)
    basis_frames = orthonormal(gram_frames, start_frames) * keep_frames[None, :]
    basis_sends = orthonormal(gram_sends, start_sends) * keep_sends[None, :]
    reduced = jnp.dot(flattened, basis_frames, precision=high).reshape(pixels, NK, TMAX)
    core = jnp.einsum("pkb,ka->pab", reduced, basis_sends, precision=high)
    core = core.reshape(rows_dev, cols_dev, CORE_W)
    gathered = lax.all_gather(core, "row", axis=0, tiled=True)
    total_rows = gathered.shape[0]
    unfolded = gathered.reshape(total_rows, -1)
    local_rows = jnp.dot(unfolded, unfolded.T, precision=high)
    gram_rows = lax.psum(local_rows, "col")
    basis_rows = orthonormal(gram_rows, start_rows)
    second = jnp.dot(basis_rows.T, unfolded, precision=high).reshape(RS, cols_dev, CORE_W)
    width = CORE_W // lax.axis_size("row")
    own_slice = lax.dynamic_slice_in_dim(second, lax.axis_index("row") * width, width, 2)
    across = lax.all_gather(own_slice, "col", axis=1, tiled=True)
    local_cols = jnp.einsum("sce,sde->cd", across, across, precision=high)
    gram_cols = lax.psum(local_cols, "row")
    basis_cols = orthonormal(gram_cols, start_cols)
    third_slice = jnp.einsum("cu,sce->sue", basis_cols, across, precision=high)
    third = lax.all_gather(third_slice, "row", axis=2, tiled=True)
    cols_own = lax.dynamic_slice_in_dim(basis_cols, lax.axis_index("col") * cols_dev, cols_dev, 0)
    rows_own = lax.dynamic_slice_in_dim(basis_rows, lax.axis_index("row") * rows_dev, rows_dev, 0)
    back_cols = jnp.einsum("cu,sue->sce", cols_own, third, precision=high)
    tissue_core = jnp.dot(rows_own, back_cols.reshape(RS, -1), precision=high)
    tissue_core = tissue_core.reshape(pixels, KMAX, TMAX)
    expanded = jnp.einsum("pab,ka->pkb", tissue_core, basis_sends, precision=high)
    tissue = jnp.dot(expanded.reshape(-1, TMAX), basis_frames.T, precision=high).reshape(
        signal.shape
    )
    return signal - tissue


def solution(mesh):
    return jax.shard_map(
        local,
        mesh=mesh,
        in_specs=(P("row", "col", None, None), P(), P(), P(), P(), P(), P()),
        out_specs=P("row", "col", None, None),
        check_vma=False,
    )
```

profile of v0, /device:TPU:0, one launch (start us, length us, event | category | flops | bytes accessed | tf_op | source)
XLA Modules:
  0.0 528.9 jit_solution(3371056779634263745)
XLA Ops:
  6.5 17.7 %convolution_bitcast_fusion.4 = f32[256,256]{1,0:T(8,128)} fusion(f32[16,32,16,256]{3,2,1,0:T(8,128)} %param.16), kind=kOutput, calls=%fused_computation.9 | convolution fusion | flops 6442450944 | bytes 8650752 | tf_op jit(solution)/shard_map/pt,pu->tu/dot_general | solution.py:32
  24.3 14.1 %convolution_bitcast_fusion.6 = f32[16,16]{1,0:T(8,128)S(1)} fusion(f32[16,32,16,256]{3,2,1,0:T(8,128)} %param.16), kind=kOutput, calls=%fused_computation.13 | convolution fusion | flops 402653184 | bytes 8389632 | tf_op jit(solution)/shard_map/pkt,pjt->kj/dot_general | solution.py:33
  39.8 42.4 %psum.28 = f32[16,16]{1,0:T(8,128)S(1)} all-reduce(f32[16,16]{1,0:T(8,128)S(1)} %convolution_bitcast_fusion.6), channel_id=1, replica_groups=mesh['row'=8,'col'=4] {'row','col'}, use_global_device_ids=true, to_apply=%region_0.0 | all-reduce | flops 256 | bytes 2048 | tf_op jit(solution)/shard_map/psum | solution.py:34
  88.6 65.3 %all-reduce.4.cloned.1.call-done = f32[256,256]{1,0:T(8,128)} async-done(((f32[256,256]{1,0:T(8,128)}), f32[256,256]{1,0:T(8,128)}) %all-reduce.4.cloned.1.call-update) | async-done | bytes 262160 | tf_op jit(solution)/shard_map/psum | solution.py:34
  170.9 9.9 %convolution_bitcast_fusion = f32[8192,32]{0,1:T(8,128)S(1)} fusion(f32[32,256]{1,0:T(8,128)S(1)} %convolution_multiply_fusion, f32[8192,256]{1,0:T(8,128)} %bitcast.199), kind=kOutput, calls=%fused_computation | convolution fusion | flops 805306368 | bytes 9469952 | tf_op jit(solution)/shard_map/dot_general | solution.py:39
  190.2 35.5 %all-gather.4.cloned.1.call-done = f32[128,32,256]{2,0,1:T(8,128)} async-done(((f32[16,32,256]{2,0,1:T(8,128)}), f32[128,32,256]{2,0,1:T(8,128)}) %all-gather.4.cloned.1.call-update) | async-done | bytes 4194320 | tf_op jit(solution)/shard_map/all_gather | solution.py:42
  225.7 7.6 %convolution_bitcast_fusion.5 = f32[128,128]{1,0:T(8,128)} fusion(f32[128,32,256]{2,0,1:T(8,128)} %all-gather.4.cloned.1.call-done), kind=kOutput, calls=%fused_computation.11 | convolution fusion | flops 1610612736 | bytes 4259840 | tf_op jit(solution)/shard_map/dot_general | solution.py:45
  233.4 5.6 %copy.60 = f32[128,32,256]{0,2,1:T(8,128)} copy(f32[128,32,256]{2,0,1:T(8,128)} %all-gather.4.cloned.1.call-done) | data formatting | bytes 8388608 | tf_op jit(solution)/shard_map/all_gather | solution.py:42
  239.0 28.8 %all-reduce.6.cloned.1.call-done = f32[128,128]{1,0:T(8,128)} async-done(((f32[128,128]{1,0:T(8,128)}), f32[128,128]{1,0:T(8,128)}) %all-reduce.6.cloned.1.call-update) | async-done | bytes 65552 | tf_op jit(solution)/shard_map/psum | solution.py:46
  269.2 5.8 %cholesky.202 = f32[64,64]{1,0:T(8,128)S(1)} custom-call(f32[64,64]{1,0:T(8,128)S(1)} %fusion.32), custom_call_target="Cholesky" | custom-call | tf_op jit(solution)/shard_map/jit(cholesky)/cholesky | solution.py:21
  276.5 4.9 custom-call.24
  283.0 5.8 %cholesky.213 = f32[64,64]{1,0:T(8,128)S(1)} custom-call(f32[64,64]{1,0:T(8,128)S(1)} %fusion.28), custom_call_target="Cholesky" | custom-call | tf_op jit(solution)/shard_map/jit(cholesky)/cholesky | solution.py:21
  290.3 4.9 custom-call.25
  295.5 5.4 %fusion = f32[64,32,256]{0,2,1:T(8,128)S(1)} fusion(f32[128,32,256]{0,2,1:T(8,128)} %copy.60, f32[64,128]{1,0:T(8,128)S(1)} %fusion.25), kind=kOutput, calls=%fused_computation.1 | convolution fusion | flops 805306368 | bytes 6324224 | tf_op jit(solution)/shard_map/dot_general | solution.py:48
  302.2 45.0 %all-gather.6.cloned.1.call-done = f32[64,128,32]{0,2,1:T(8,128)} async-done(((f32[64,32,32]{0,2,1:T(8,128)}), f32[64,128,32]{0,2,1:T(8,128)}) %all-gather.6.cloned.1.call-update) | async-done | bytes 1048592 | tf_op jit(solution)/shard_map/all_gather | solution.py:51
  347.2 7.0 %fusion.4 = f32[128,128]{1,0:T(8,128)} fusion(f32[64,128,32]{0,2,1:T(8,128)} %all-gather.6.cloned.1.call-done), kind=kOutput, calls=%fused_computation.10 | convolution fusion | flops 402653184 | bytes 1114112 | tf_op jit(solution)/shard_map/sce,sde->cd/dot_general | solution.py:52
  357.4 49.1 %all-reduce.8.cloned.1.call-done = f32[128,128]{1,0:T(8,128)} async-done(((f32[128,128]{1,0:T(8,128)}), f32[128,128]{1,0:T(8,128)}) %all-reduce.8.cloned.1.call-update) | async-done | bytes 65552 | tf_op jit(solution)/shard_map/psum | solution.py:53
  407.8 5.8 %cholesky.224 = f32[64,64]{1,0:T(8,128)S(1)} custom-call(f32[64,64]{1,0:T(8,128)S(1)} %fusion.23), custom_call_target="Cholesky" | custom-call | tf_op jit(solution)/shard_map/jit(cholesky)/cholesky | solution.py:21
  415.0 4.9 custom-call.26
  421.5 5.8 %cholesky.235 = f32[64,64]{1,0:T(8,128)S(1)} custom-call(f32[64,64]{1,0:T(8,128)S(1)} %fusion.19), custom_call_target="Cholesky" | custom-call | tf_op jit(solution)/shard_map/jit(cholesky)/cholesky | solution.py:21
  428.7 4.9 custom-call.27
  435.8 53.8 %all-gather.8.cloned.1.call-done = f32[64,64,256]{1,2,0:T(8,128)} async-done(((f32[64,64,32]{1,2,0:T(8,128)}), f32[64,64,256]{1,2,0:T(8,128)}) %all-gather.8.cloned.1.call-update) | async-done | bytes 4194320 | tf_op jit(solution)/shard_map/all_gather | solution.py:56
  489.6 11.5 %fusion.13 = f32[64,256,32]{1,2,0:T(8,128)S(1)} fusion(f32[64,64,256]{1,2,0:T(8,128)} %all-gather.8.cloned.1.call-done, f32[64,128]{1,0:T(8,128)S(1)} %fusion.16, s32[]{:T(128)S(6)} %select_n.20), kind=kOutput, calls=%fused_computation.25 | convolution fusion | flops 402653184 | bytes 6324228 | tf_op jit(solution)/shard_map/cu,sue->sce/dot_general | solution.py:59
  510.0 11.8 %convolution_subtract_fusion = f32[16,32,16,256]{3,2,1,0:T(8,128)} fusion(f32[16,32,16,256]{3,2,1,0:T(8,128)} %param.16, f32[16,32,16,32]{3,2,1,0:T(8,128)} %bitcast.200, f32[32,256]{1,0:T(8,128)S(1)} %convolution_multiply_fusion), kind=kOutput, calls=%fused_computation.3 | convolution fusion | flops 807403520 | bytes 17858560 | tf_op jit(solution)/shard_map/dot_general | solution.py:63
  (111 shorter events, 60.0 us)
Async XLA Ops:
  6.5 147.4 %copy-start = (f32[256,32]{0,1:T(8,128)S(1)}, f32[256,32]{0,1:T(8,128)}, u32[]{:S(2)}) copy-start(f32[256,32]{0,1:T(8,128)} %param.17) | copy-start | bytes 98308
  6.5 147.4 %all-reduce.4.cloned.1.call-start = ((), (), s32[]{:S(2)}) async-start(), calls=%async_computation | async-start | bytes 524288 | tf_op jit(solution)/shard_map/psum | solution.py:34
  24.3 57.9 %copy-start.4 = (f32[16,8]{0,1:T(8,128)S(1)}, f32[16,8]{0,1:T(8,128)}, u32[]{:S(2)}) copy-start(f32[16,8]{0,1:T(8,128)} %param.18) | copy-start | bytes 1540
  24.3 201.5 %all-gather.4.cloned.1.call-start = ((), (), s32[]{:S(2)}) async-start(), calls=%async_computation.1 | async-start | bytes 4718592 | tf_op jit(solution)/shard_map/all_gather | solution.py:42
  189.9 77.9 %all-reduce.6.cloned.1.call-start = ((), (), s32[]{:S(2)}) async-start(), calls=%async_computation.2 | async-start | bytes 131072 | tf_op jit(solution)/shard_map/psum | solution.py:46
  233.3 113.9 %all-gather.6.cloned.1.call-start = ((), (), s32[]{:S(2)}) async-start(), calls=%async_computation.3 | async-start | bytes 2621440 | tf_op jit(solution)/shard_map/all_gather | solution.py:51
  233.4 34.4 %copy-start.2 = (f32[128,64]{0,1:T(8,128)S(1)}, f32[128,64]{0,1:T(8,128)}, u32[]{:S(2)}) copy-start(f32[128,64]{0,1:T(8,128)} %param.19) | copy-start | bytes 98308
  300.9 105.6 %copy-start.3 = (f32[128,64]{0,1:T(8,128)S(1)}, f32[128,64]{0,1:T(8,128)}, u32[]{:S(2)}) copy-start(f32[128,64]{0,1:T(8,128)} %param.20) | copy-start | bytes 98308
  301.7 104.7 %all-reduce.8.cloned.1.call-start = ((), (), s32[]{:S(2)}) async-start(), calls=%async_computation.4 | async-start | bytes 131072 | tf_op jit(solution)/shard_map/psum | solution.py:53
  354.3 135.3 %all-gather.8.cloned.1.call-start = ((), (), s32[]{:S(2)}) async-start(), calls=%async_computation.5 | async-start | bytes 9437184 | tf_op jit(solution)/shard_map/all_gather | solution.py:56
  510.0 11.8 %copy-start.1 = (f32[256,32]{0,1:T(8,128)S(1)}, f32[256,32]{0,1:T(8,128)}, u32[]{:S(2)}) copy-start(f32[256,32]{0,1:T(8,128)} %param.17) | copy-start | bytes 98308
Sparse Core Ops, SparseCore 0:
  24.4 129.5 all-reduce.3
  190.1 35.6 all-gather.3
  233.5 34.2 all-reduce.5
  301.9 45.3 all-gather.5
  354.4 51.9 all-reduce.7
  435.9 53.6 all-gather.7
where the time goes:
time: 537 us; the launch traced here: 529 us
  waiting for transfers between devices  278 us (52%)
  matrix products  100 us (19%)
  other arithmetic  67.3 us (13%)
  blocking collectives  42.4 us (8%)
  local copies, waits for them, and re-layouts  25.1 us (5%)
  between operations  15.5 us (3%)
    psum x1, waiting for transfers between devices, local(): lax.psum((local_frames, local_sends), ('row', 'col'))  65.3 us
    all_gather x1, waiting for transfers between devices, local(): third = lax.all_gather(third_slice, 'row', axis=2, tiled=True)  53.8 us
    psum x1, waiting for transfers between devices, local(): gram_cols = lax.psum(local_cols, 'row')  49.1 us
    all_gather x1, waiting for transfers between devices, local(): across = lax.all_gather(own_slice, 'col', axis=1, tiled=True)  45 us
    psum x1, blocking collectives, local(): lax.psum((local_frames, local_sends), ('row', 'col'))  42.4 us
    another operation x24, other arithmetic, orthonormal(): factor = jnp.linalg.cholesky(inner)  36.3 us
    all_gather x1, waiting for transfers between devices, local(): gathered = lax.all_gather(core, 'row', axis=0, tiled=True)  35.5 us
    another operation x16, other arithmetic, orthonormal(): basis = jax.scipy.linalg.solve_triangular(factor, image.T, lower=True).T  31 us
  transfers between devices with their start and end apart: 6, of which 6 were waited for; matrix products, arithmetic and copies ran while one was open for 6% of the time, Pallas kernels for 0%

commit v1 on v0

--- a/solution.py
+++ b/solution.py
@@ -43,7 +43,7 @@
     total_rows = gathered.shape[0]
     unfolded = gathered.reshape(total_rows, -1)
     local_rows = jnp.dot(unfolded, unfolded.T, precision=high)
-    gram_rows = lax.psum(local_rows, "col")
+    gram_rows = jnp.sum(lax.all_gather(local_rows, "col"), axis=0)
     basis_rows = orthonormal(gram_rows, start_rows)
     second = jnp.dot(basis_rows.T, unfolded, precision=high).reshape(RS, cols_dev, CORE_W)
     width = CORE_W // lax.axis_size("row")

time: 537 us -> 520 us (0.968)
  waiting for transfers between devices: 278 us -> 250 us
  blocking collectives: 42.4 us -> 56.3 us
    psum x1 -> x0, waiting for transfers between devices: 28.8 us -> none  [local(): gram_rows = lax.psum(local_rows, 'col')]
    all_gather x0 -> x1, blocking collectives: none -> 13.9 us  [local(): gram_rows = jnp.sum(lax.all_gather(local_rows, 'col'), axis=0)]
  transfers between devices with their start and end apart: 6 -> 5, of which waited for: 6 -> 5; matrix products, arithmetic and copies ran while one was open for 6% -> 5% of each run, Pallas kernels for 0% -> 0%
where the time goes in v1:
time: 520 us; the launch traced here: 512 us
  waiting for transfers between devices  250 us (48%)
  matrix products  97.8 us (19%)
  other arithmetic  67.1 us (13%)
  blocking collectives  56.3 us (11%)
  local copies, waits for them, and re-layouts  25.1 us (5%)
  between operations  15.1 us (3%)
    psum x1, waiting for transfers between devices, local(): lax.psum((local_frames, local_sends), ('row', 'col'))  65.3 us
    all_gather x1, waiting for transfers between devices, local(): third = lax.all_gather(third_slice, 'row', axis=2, tiled=True)  53.8 us
    psum x1, waiting for transfers between devices, local(): gram_cols = lax.psum(local_cols, 'row')  49.1 us
    all_gather x1, waiting for transfers between devices, local(): across = lax.all_gather(own_slice, 'col', axis=1, tiled=True)  45.9 us
    psum x1, blocking collectives, local(): lax.psum((local_frames, local_sends), ('row', 'col'))  42.4 us
    another operation x24, other arithmetic, orthonormal(): factor = jnp.linalg.cholesky(inner)  36.1 us
    all_gather x1, waiting for transfers between devices, local(): gathered = lax.all_gather(core, 'row', axis=0, tiled=True)  35.5 us
    another operation x16, other arithmetic, orthonormal(): basis = jax.scipy.linalg.solve_triangular(factor, image.T, lower=True).T  30.9 us
  transfers between devices with their start and end apart: 5, of which 5 were waited for; matrix products, arithmetic and copies ran while one was open for 5% of the time, Pallas kernels for 0%

profile of v1, /device:TPU:0, one launch (start us, length us, event | category | flops | bytes accessed | tf_op | source)
XLA Modules:
  0.0 511.9 jit_solution(5196639394590275542)
XLA Ops:
  6.5 17.7 %convolution_bitcast_fusion.4 = f32[256,256]{1,0:T(8,128)} fusion(f32[16,32,16,256]{3,2,1,0:T(8,128)} %param.16), kind=kOutput, calls=%fused_computation.9 | convolution fusion | flops 6442450944 | bytes 8650752 | tf_op jit(solution)/shard_map/pt,pu->tu/dot_general | solution.py:32
  24.3 14.1 %convolution_bitcast_fusion.6 = f32[16,16]{1,0:T(8,128)S(1)} fusion(f32[16,32,16,256]{3,2,1,0:T(8,128)} %param.16), kind=kOutput, calls=%fused_computation.13 | convolution fusion | flops 402653184 | bytes 8389632 | tf_op jit(solution)/shard_map/pkt,pjt->kj/dot_general | solution.py:33
  39.8 42.4 %psum.21 = f32[16,16]{1,0:T(8,128)S(1)} all-reduce(f32[16,16]{1,0:T(8,128)S(1)} %convolution_bitcast_fusion.6), channel_id=1, replica_groups=mesh['row'=8,'col'=4] {'row','col'}, use_global_device_ids=true, to_apply=%region_0.0 | all-reduce | flops 256 | bytes 2048 | tf_op jit(solution)/shard_map/psum | solution.py:34
  88.6 65.3 %all-reduce.3.cloned.1.call-done = f32[256,256]{1,0:T(8,128)} async-done(((f32[256,256]{1,0:T(8,128)}), f32[256,256]{1,0:T(8,128)}) %all-reduce.3.cloned.1.call-update) | async-done | bytes 262160 | tf_op jit(solution)/shard_map/psum | solution.py:34
  170.9 9.9 %convolution_bitcast_fusion = f32[8192,32]{0,1:T(8,128)S(1)} fusion(f32[32,256]{1,0:T(8,128)S(1)} %convolution_multiply_fusion, f32[8192,256]{1,0:T(8,128)} %bitcast.200), kind=kOutput, calls=%fused_computation | convolution fusion | flops 805306368 | bytes 9469952 | tf_op jit(solution)/shard_map/dot_general | solution.py:39
  190.2 35.5 %all-gather.5.cloned.1.call-done = f32[128,32,256]{2,0,1:T(8,128)} async-done(((f32[16,32,256]{2,0,1:T(8,128)}), f32[128,32,256]{2,0,1:T(8,128)}) %all-gather.5.cloned.1.call-update) | async-done | bytes 4194320 | tf_op jit(solution)/shard_map/all_gather | solution.py:42
  225.7 6.9 %convolution_bitcast_fusion.5 = f32[128,128]{1,0:T(8,128)S(1)} fusion(f32[128,32,256]{2,0,1:T(8,128)} %all-gather.5.cloned.1.call-done), kind=kOutput, calls=%fused_computation.11 | convolution fusion | flops 1610612736 | bytes 4259840 | tf_op jit(solution)/shard_map/dot_general | solution.py:45
  232.7 13.9 %all-gather = f32[512,128]{1,0:T(8,128)S(1)} all-gather(f32[128,128]{1,0:T(8,128)S(1)} %convolution_bitcast_fusion.5), channel_id=2, replica_groups=mesh['row'=8,'col'=4] {'col'}, dimensions={0}, use_global_device_ids=true | all-gather | bytes 327680 | tf_op jit(solution)/shard_map/all_gather | solution.py:46
  247.2 5.8 %cholesky.202 = f32[64,64]{1,0:T(8,128)S(1)} custom-call(f32[64,64]{1,0:T(8,128)S(1)} %fusion.32), custom_call_target="Cholesky" | custom-call | tf_op jit(solution)/shard_map/jit(cholesky)/cholesky | solution.py:21
  254.4 4.9 custom-call.24
  260.1 5.8 %cholesky.213 = f32[64,64]{1,0:T(8,128)S(1)} custom-call(f32[64,64]{1,0:T(8,128)S(1)} %fusion.28), custom_call_target="Cholesky" | custom-call | tf_op jit(solution)/shard_map/jit(cholesky)/cholesky | solution.py:21
  267.3 4.9 custom-call.25
  272.4 5.6 %copy.60 = f32[128,32,256]{0,2,1:T(8,128)} copy(f32[128,32,256]{2,0,1:T(8,128)} %all-gather.5.cloned.1.call-done) | data formatting | bytes 8388608 | tf_op jit(solution)/shard_map/all_gather | solution.py:42
  278.0 5.4 %fusion = f32[64,32,256]{0,2,1:T(8,128)S(1)} fusion(f32[128,32,256]{0,2,1:T(8,128)} %copy.60, f32[64,128]{1,0:T(8,128)S(1)} %fusion.25), kind=kOutput, calls=%fused_computation.1 | convolution fusion | flops 805306368 | bytes 6324224 | tf_op jit(solution)/shard_map/dot_general | solution.py:48
  284.7 45.9 %all-gather.7.cloned.1.call-done = f32[64,128,32]{0,2,1:T(8,128)} async-done(((f32[64,32,32]{0,2,1:T(8,128)}), f32[64,128,32]{0,2,1:T(8,128)}) %all-gather.7.cloned.1.call-update) | async-done | bytes 1048592 | tf_op jit(solution)/shard_map/all_gather | solution.py:51
  330.6 7.0 %fusion.4 = f32[128,128]{1,0:T(8,128)} fusion(f32[64,128,32]{0,2,1:T(8,128)} %all-gather.7.cloned.1.call-done), kind=kOutput, calls=%fused_computation.10 | convolution fusion | flops 402653184 | bytes 1114112 | tf_op jit(solution)/shard_map/sce,sde->cd/dot_general | solution.py:52
  340.7 49.1 %all-reduce.5.cloned.1.call-done = f32[128,128]{1,0:T(8,128)} async-done(((f32[128,128]{1,0:T(8,128)}), f32[128,128]{1,0:T(8,128)}) %all-reduce.5.cloned.1.call-update) | async-done | bytes 65552 | tf_op jit(solution)/shard_map/psum | solution.py:53
  391.1 5.8 %cholesky.224 = f32[64,64]{1,0:T(8,128)S(1)} custom-call(f32[64,64]{1,0:T(8,128)S(1)} %fusion.23), custom_call_target="Cholesky" | custom-call | tf_op jit(solution)/shard_map/jit(cholesky)/cholesky | solution.py:21
  398.3 4.9 custom-call.26
  404.9 5.8 %cholesky.235 = f32[64,64]{1,0:T(8,128)S(1)} custom-call(f32[64,64]{1,0:T(8,128)S(1)} %fusion.19), custom_call_target="Cholesky" | custom-call | tf_op jit(solution)/shard_map/jit(cholesky)/cholesky | solution.py:21
  412.0 4.9 custom-call.27
  419.2 53.8 %all-gather.9.cloned.1.call-done = f32[64,64,256]{1,2,0:T(8,128)} async-done(((f32[64,64,32]{1,2,0:T(8,128)}), f32[64,64,256]{1,2,0:T(8,128)}) %all-gather.9.cloned.1.call-update) | async-done | bytes 4194320 | tf_op jit(solution)/shard_map/all_gather | solution.py:56
  473.0 11.5 %fusion.13 = f32[64,256,32]{1,2,0:T(8,128)S(1)} fusion(f32[64,64,256]{1,2,0:T(8,128)} %all-gather.9.cloned.1.call-done, f32[64,128]{1,0:T(8,128)S(1)} %fusion.16, s32[]{:T(128)S(6)} %select_n.20), kind=kOutput, calls=%fused_computation.25 | convolution fusion | flops 402653184 | bytes 6324228 | tf_op jit(solution)/shard_map/cu,sue->sce/dot_general | solution.py:59
  493.3 11.8 %convolution_subtract_fusion = f32[16,32,16,256]{3,2,1,0:T(8,128)} fusion(f32[16,32,16,256]{3,2,1,0:T(8,128)} %param.16, f32[16,32,16,32]{3,2,1,0:T(8,128)} %bitcast.201, f32[32,256]{1,0:T(8,128)S(1)} %convolution_multiply_fusion), kind=kOutput, calls=%fused_computation.3 | convolution fusion | flops 807403520 | bytes 17858560 | tf_op jit(solution)/shard_map/dot_general | solution.py:63
  (110 shorter events, 58.0 us)
Async XLA Ops:
  6.5 147.4 %copy-start = (f32[256,32]{0,1:T(8,128)S(1)}, f32[256,32]{0,1:T(8,128)}, u32[]{:S(2)}) copy-start(f32[256,32]{0,1:T(8,128)} %param.17) | copy-start | bytes 98308
  6.5 147.4 %all-reduce.3.cloned.1.call-start = ((), (), s32[]{:S(2)}) async-start(), calls=%async_computation | async-start | bytes 524288 | tf_op jit(solution)/shard_map/psum | solution.py:34
  24.3 57.9 %copy-start.4 = (f32[16,8]{0,1:T(8,128)S(1)}, f32[16,8]{0,1:T(8,128)}, u32[]{:S(2)}) copy-start(f32[16,8]{0,1:T(8,128)} %param.18) | copy-start | bytes 1540
  24.3 201.5 %all-gather.5.cloned.1.call-start = ((), (), s32[]{:S(2)}) async-start(), calls=%async_computation.1 | async-start | bytes 4718592 | tf_op jit(solution)/shard_map/all_gather | solution.py:42
  189.9 140.6 %all-gather.7.cloned.1.call-start = ((), (), s32[]{:S(2)}) async-start(), calls=%async_computation.2 | async-start | bytes 2621440 | tf_op jit(solution)/shard_map/all_gather | solution.py:51
  190.2 56.4 %copy-start.2 = (f32[128,64]{0,1:T(8,128)S(1)}, f32[128,64]{0,1:T(8,128)}, u32[]{:S(2)}) copy-start(f32[128,64]{0,1:T(8,128)} %param.19) | copy-start | bytes 98308
  283.4 106.4 %copy-start.3 = (f32[128,64]{0,1:T(8,128)S(1)}, f32[128,64]{0,1:T(8,128)}, u32[]{:S(2)}) copy-start(f32[128,64]{0,1:T(8,128)} %param.20) | copy-start | bytes 98308
  284.2 105.5 %all-reduce.5.cloned.1.call-start = ((), (), s32[]{:S(2)}) async-start(), calls=%async_computation.3 | async-start | bytes 131072 | tf_op jit(solution)/shard_map/psum | solution.py:53
  337.6 135.3 %all-gather.9.cloned.1.call-start = ((), (), s32[]{:S(2)}) async-start(), calls=%async_computation.4 | async-start | bytes 9437184 | tf_op jit(solution)/shard_map/all_gather | solution.py:56
  493.3 11.8 %copy-start.1 = (f32[256,32]{0,1:T(8,128)S(1)}, f32[256,32]{0,1:T(8,128)}, u32[]{:S(2)}) copy-start(f32[256,32]{0,1:T(8,128)} %param.17) | copy-start | bytes 98308
Sparse Core Ops, SparseCore 0:
  24.4 129.5 all-reduce.2
  190.1 35.6 all-gather.4
  284.4 46.1 all-gather.6
  337.8 51.9 all-reduce.4
  419.3 53.6 all-gather.8
